TPU v7x, 32 devices: a whole 2x2x4 slice. The times are simulated.
32 devices in a mesh: aa: 4 (over x, core), ba: 8 (over z, y).
Axes of the slice: x: 2, y: 2, z: 4, core: 2. Of those that a mesh axis runs over, the one named last changes fastest.
Arguments:
- head_outputs: bfloat16 [1024, 4096], P('ba'), may hold values from -6 to 6
- stream: bfloat16 [1024, 4096], P('ba'), may hold values from -6 to 6
- adapter_down_factors: bfloat16 [4096, 512], P(None, 'aa'), may hold values from -0.09375 to 0.09375
- adapter_up_factors: bfloat16 [512, 4096], P('aa'), may hold values from -1.5 to 1.5
- norm_gain_vector: float32 [4096], replicated, may hold values from 0.5 to 1.5
- router_matrix: bfloat16 [4096, 8], replicated, may hold values from -0.09375 to 0.09375
- token_adapter_index: int32 [1024], P('ba'), may hold values from 0 to 31
- token_expert_index: int32 [1024, 2], P('ba'), may hold values from 0 to 7, all different within a row; in each aligned block of 128 rows (0 to 127, 128 to 255, ...) at most 48 rows name the same one
- gate_weight: bfloat16 [8, 4096, 14336], P('ba', None, 'aa'), may hold values from -0.09375 to 0.09375
- up_weight: bfloat16 [8, 4096, 14336], P('ba', None, 'aa'), may hold values from -0.09375 to 0.09375
- down_weight: bfloat16 [8, 14336, 4096], P('ba', 'aa'), may hold values from -0.046875 to 0.046875
Outputs:
- mixed: bfloat16 [1024, 4096], P('ba', 'aa')
- adapter_load: float32 [32], P('aa')
Inputs may be any that keep to these rules, and one draw needn't show every extreme that they name: `token_expert_index`: the two experts of a row differ; in each aligned block of 128 rows no expert is named by more than 48 rows.
All inputs are finite; a program needn't handle non-finite values.
Results may differ from a plain program's by a relative error of at most 0.0049.
Values may be sent and summed in bfloat16 or wider, within the bound.
A program may use at most 192 MiB of HBM per device.

v0:
```python
import functools

import jax
import jax.numpy as jnp
from jax import lax
from jax.experimental import pallas as pl
from jax.experimental.pallas import tpu as pltpu
from jax.sharding import PartitionSpec as P

E = 8
ADAPTER_RANK = 16
CAP = 48
CORES = 2

EPS = 1e-05
ADAPTER_SCALE = 2.0
MESH = pl.DeviceIdType.MESH
F32 = jnp.float32
BF16 = jnp.bfloat16


def cols(block, width):
    return pl.ds(pl.multiple_of(block * width, 128), width)


def greet(places):
    barrier = pltpu.get_barrier_semaphore()
    for place in places:
        pl.semaphore_signal(barrier, inc=1, device_id=place, device_id_type=MESH)
    pl.semaphore_wait(barrier, len(places))


def send(src, dst, send_sem, recv_sem, place):
    copy = pltpu.make_async_remote_copy(
        src_ref=src,
        dst_ref=dst,
        send_sem=send_sem,
        recv_sem=recv_sem,
        device_id=place,
        device_id_type=MESH,
    )
    copy.start()
    return copy


def peers(axis, me, n):
    return [{axis: lax.rem(me + k, n)} for k in range(1, n)]


def front(
    n_aa, n_ba, model_width,
    idx_ref, idxt_ref, head_ref, stream_ref, down_ref, gain_ref, router_ref, up_ref,
    x_ref, res_ref, logit_ref, load_ref,
    up_all, low_all, sq_all, lg_all, ld_all, outgoing,
    own_sem, up_s, up_r, low_s, low_r, sq_s, sq_r, lg_s, lg_r, ld_s, ld_r,
    ba_s, ba_r, xg_s, xg_r, cg_s, cg_r,
):
    aa, ba = lax.axis_index("aa"), lax.axis_index("ba")
    nx = n_aa // CORES
    x, core = aa // CORES, lax.rem(aa, CORES)
    partner = {"aa": x * CORES + 1 - core}
    toks = head_ref.shape[0]
    held = down_ref.shape[1]
    width = model_width // n_aa
    halves = n_ba // E
    aa_peers, ba_peers = peers("aa", aa, n_aa), peers("ba", ba, n_ba)
    greet(aa_peers + ba_peers)
    pending = []

    def fan(places, src, dst, s, r):
        copies = [send(src, dst, s.at[i], r.at[i], p) for i, p in enumerate(places)]
        pending.extend(copies)
        return copies

    up_copies = []
    for k in range(1, n_aa):
        to = lax.rem(aa + k, n_aa)
        up_copies.append(send(
            up_ref.at[:, cols(to, width)], up_all.at[aa], up_s.at[k - 1], up_r.at[k - 1], {"aa": to}
        ))
    pending.extend(up_copies)
    own_up = pltpu.make_async_copy(up_ref.at[:, cols(aa, width)], up_all.at[aa], own_sem)
    own_up.start()

    local = idx_ref[:, 2:3] - aa * (held // ADAPTER_RANK)
    lanes = lax.broadcasted_iota(jnp.int32, (toks, held), 1)
    projected = jnp.dot(head_ref[...], down_ref[...], preferred_element_type=F32)
    low_all[aa] = jnp.where(local == lanes // ADAPTER_RANK, projected, 0.0).astype(BF16)
    low_copies = fan(aa_peers, low_all.at[aa], low_all.at[aa], low_s, low_r)

    tally = jnp.sum((local == lanes).astype(F32), axis=0, keepdims=True)
    ld_all[ba] = jnp.broadcast_to(tally, ld_all.shape[1:])
    ld_copies = fan(ba_peers, ld_all.at[ba], ld_all.at[ba], ld_s, ld_r)

    experts = lax.broadcasted_iota(jnp.int32, (E, toks), 0)
    hits = ((idxt_ref[0:1, :] == experts) | (idxt_ref[1:2, :] == experts)).astype(F32)
    earlier = (
        lax.broadcasted_iota(jnp.int32, (toks, toks), 0)
        < lax.broadcasted_iota(jnp.int32, (toks, toks), 1)
    ).astype(F32)
    place = jnp.dot(hits.astype(BF16), earlier.astype(BF16), preferred_element_type=F32)
    place = jnp.where(hits > 0.0, place, -1.0).astype(jnp.int32)
    spots = lax.broadcasted_iota(jnp.int32, (CAP, toks), 0)

    own_up.wait()
    for copy in low_copies + up_copies:
        copy.wait_recv()
    delta = jnp.dot(low_all[0], up_all[0], preferred_element_type=F32)
    for j in range(1, n_aa):
        delta = delta + jnp.dot(low_all[j], up_all[j], preferred_element_type=F32)
    residual = stream_ref[:, cols(aa, width)].astype(F32) + ADAPTER_SCALE * delta
    res_ref[...] = residual
    square = jnp.sum(residual * residual, axis=1, keepdims=True)
    sq_all[aa] = jnp.broadcast_to(square, sq_all.shape[1:])
    for copy in fan(aa_peers, sq_all.at[aa], sq_all.at[aa], sq_s, sq_r):
        copy.wait_recv()
    total = sq_all[0]
    for j in range(1, n_aa):
        total = total + sq_all[j]
    inv_norm = lax.rsqrt(total[:, 0:1] / model_width + EPS)
    normed = (res_ref[...] * inv_norm * gain_ref[:, cols(aa, width)]).astype(BF16)

    for e in range(E):
        pick = (place[e : e + 1, :] == spots).astype(F32).astype(BF16)
        rows = jnp.dot(pick, normed, preferred_element_type=F32).astype(BF16)
        for j in range(halves):
            outgoing[e * halves + j] = rows
    mine = cols(aa, width)
    ba_copies = []
    for k in range(1, n_ba):
        to = lax.rem(ba + k, n_ba)
        ba_copies.append(send(
            outgoing.at[to], x_ref.at[ba, :, mine], ba_s.at[k - 1], ba_r.at[k - 1], {"ba": to}
        ))
    pending.extend(ba_copies)
    x_ref[ba, :, mine] = outgoing[ba]

    part = jnp.dot(
        normed,
        router_ref[pl.ds(pl.multiple_of(aa * width, 128), width), :],
        preferred_element_type=F32,
    )
    lg_all[aa] = part
    lg_copies = fan(aa_peers, lg_all.at[aa], lg_all.at[aa], lg_s, lg_r)

    x_copies, c_copies = [], []
    for k in range(n_ba):
        source = lax.rem(ba - k + n_ba, n_ba)
        if k:
            ba_copies[k - 1].wait_recv()
        block = x_ref.at[source, :, mine]
        for kx in range(1, nx):
            to = lax.rem(x + kx, nx) * CORES + core
            i = k * (nx - 1) + kx - 1
            x_copies.append(send(block, block, xg_s.at[i], xg_r.at[i], {"aa": to}))
        c_copies.append(send(block, block, cg_s.at[k * nx], cg_r.at[k * nx], partner))
    for k in range(n_ba):
        source = lax.rem(ba - k + n_ba, n_ba)
        for kx in range(1, nx):
            x_copies[k * (nx - 1) + kx - 1].wait_recv()
            origin = lax.rem(x - kx + nx, nx) * CORES + core
            block = x_ref.at[source, :, cols(origin, width)]
            i = k * nx + kx
            c_copies.append(send(block, block, cg_s.at[i], cg_r.at[i], partner))
    pending.extend(x_copies + c_copies)

    for copy in lg_copies + ld_copies:
        copy.wait_recv()
    logits = lg_all[0]
    for j in range(1, n_aa):
        logits = logits + lg_all[j]
    logit_ref[...] = logits
    load = ld_all[0]
    for j in range(1, n_ba):
        load = load + ld_all[j]
    load_ref[...] = load
    for copy in c_copies:
        copy.wait_recv()
    for copy in pending:
        copy.wait_send()


def back(
    n_aa, n_ba,
    idx_ref, res_ref, logit_ref, y_ref,
    out_ref,
    c1, xs, c2, acc, bs, ret,
    c_s, c_r, x_s, x_r, b_s, b_r,
):
    aa, ba = lax.axis_index("aa"), lax.axis_index("ba")
    nx = n_aa // CORES
    x, core = aa // CORES, lax.rem(aa, CORES)
    partner = {"aa": x * CORES + 1 - core}
    toks, width = out_ref.shape
    halves = n_ba // E
    x_peers = [{"aa": lax.rem(x + kx, nx) * CORES + core} for kx in range(1, nx)]
    greet([partner] + x_peers + peers("ba", ba, n_ba))
    order = list(range(1, n_ba)) + [0]
    far_first = list(range(1, nx)) + [0]

    c_copies, x_copies, b_copies = {}, {}, {}
    for k in order:
        to = lax.rem(ba + k, n_ba)
        for kx in far_first:
            block = lax.rem(x + kx, nx) * CORES + 1 - core
            i = k * nx + kx
            c_copies[k, kx] = send(
                y_ref.at[to, :, cols(block, width)], c1.at[kx, k], c_s.at[i], c_r.at[i], partner
            )

    first, second = idx_ref[:, 0:1], idx_ref[:, 1:2]
    experts = lax.broadcasted_iota(jnp.int32, (toks, E), 1)
    hit0, hit1 = (first == experts).astype(F32), (second == experts).astype(F32)
    logits = logit_ref[...]
    own0 = jnp.sum(hit0 * logits, axis=1, keepdims=True)
    own1 = jnp.sum(hit1 * logits, axis=1, keepdims=True)
    weight0 = 1.0 / (1.0 + jnp.exp(own1 - own0))
    weight1 = 1.0 / (1.0 + jnp.exp(own0 - own1))
    earlier = (
        lax.broadcasted_iota(jnp.int32, (toks, toks), 1)
        < lax.broadcasted_iota(jnp.int32, (toks, toks), 0)
    ).astype(F32)
    place = jnp.dot(earlier.astype(BF16), (hit0 + hit1).astype(BF16), preferred_element_type=F32)
    spots = lax.broadcasted_iota(jnp.int32, (toks, n_ba * CAP), 1)

    def picked(expert, hit):
        spot = jnp.sum(hit * place, axis=1, keepdims=True).astype(jnp.int32)
        found = spots == expert * (halves * CAP) + spot
        for j in range(1, halves):
            found = found | (spots == (expert * halves + j) * CAP + spot)
        return found.astype(F32).astype(BF16)

    pick0, pick1 = picked(first, hit0), picked(second, hit1)

    for k in order:
        to = lax.rem(ba + k, n_ba)
        for kx in far_first:
            block = lax.rem(x + kx, nx) * CORES + core
            c_copies[k, kx].wait_recv()
            pair = y_ref[to, :, cols(block, width)].astype(F32) + c1[kx, k].astype(F32)
            if kx:
                i = k * (nx - 1) + kx - 1
                xs[kx - 1, k] = pair.astype(BF16)
                x_copies[k, kx] = send(
                    xs.at[kx - 1, k], c2.at[kx - 1, k], x_s.at[i], x_r.at[i], x_peers[kx - 1]
                )
            else:
                acc[k] = pair
    for k in order:
        total = acc[k]
        for kx in range(1, nx):
            x_copies[k, kx].wait_recv()
            total = total + c2[kx - 1, k].astype(F32)
        if k:
            bs[k - 1] = total.astype(BF16)
            b_copies[k] = send(
                bs.at[k - 1], ret.at[ba], b_s.at[k - 1], b_r.at[k - 1],
                {"ba": lax.rem(ba + k, n_ba)},
            )
        else:
            ret[ba] = total.astype(BF16)
    for k in range(1, n_ba):
        b_copies[k].wait_recv()
    rows = ret[...].reshape(n_ba * CAP, width)
    mixed = weight0 * jnp.dot(pick0, rows, preferred_element_type=F32)
    mixed = mixed + weight1 * jnp.dot(pick1, rows, preferred_element_type=F32)
    out_ref[...] = (res_ref[...] + mixed).astype(BF16)
    for copies in (c_copies, x_copies, b_copies):
        for copy in copies.values():
            copy.wait_send()


def shards(
    head_outputs,
    stream,
    adapter_down_factors,
    adapter_up_factors,
    norm_gain_vector,
    router_matrix,
    token_adapter_index,
    token_expert_index,
    gate_weight,
    up_weight,
    down_weight,
):
    toks, model_width = head_outputs.shape
    n_aa, n_ba = lax.axis_size("aa"), lax.axis_size("ba")
    nx = n_aa // CORES
    held = adapter_down_factors.shape[1]
    width = model_width // n_aa
    vmem = pl.BlockSpec(memory_space=pltpu.VMEM)
    dma = pltpu.SemaphoreType.DMA
    idx = jnp.concatenate([token_expert_index, token_adapter_index[:, None]], axis=1)

    def sems(n):
        return [dma((max(n, 1),)), dma((max(n, 1),))]

    x, residual, logits, load = pl.pallas_call(
        functools.partial(front, n_aa, n_ba, model_width),
        out_shape=(
            jax.ShapeDtypeStruct((n_ba, CAP, model_width), BF16),
            jax.ShapeDtypeStruct((toks, width), F32),
            jax.ShapeDtypeStruct((toks, E), F32),
            jax.ShapeDtypeStruct((8, held), F32),
        ),
        in_specs=[vmem] * 7 + [pl.BlockSpec(memory_space=pl.ANY)],
        out_specs=(vmem,) * 4,
        scratch_shapes=[
            pltpu.VMEM((n_aa, held, width), BF16),
            pltpu.VMEM((n_aa, toks, held), BF16),
            pltpu.VMEM((n_aa, toks, 128), F32),
            pltpu.VMEM((n_aa, toks, E), F32),
            pltpu.VMEM((n_ba, 8, held), F32),
            pltpu.VMEM((n_ba, CAP, width), BF16),
            dma,
        ]
        + sems(n_aa - 1) * 4
        + sems(n_ba - 1) * 2
        + sems(n_ba * (nx - 1))
        + sems(n_ba * nx),
        compiler_params=pltpu.CompilerParams(
            collective_id=0, has_side_effects=True, vmem_limit_bytes=48 * 2**20
        ),
        name="front",
    )(
        idx, token_expert_index.T, head_outputs, stream, adapter_down_factors,
        norm_gain_vector[None, :], router_matrix, adapter_up_factors,
    )
    rows = x.reshape(n_ba * CAP, model_width)
    gate_proj = jnp.dot(rows, gate_weight[0], preferred_element_type=F32)
    up_proj = jnp.dot(rows, up_weight[0], preferred_element_type=F32)
    hidden = (jax.nn.silu(gate_proj) * up_proj).astype(BF16)
    partial_value = jnp.dot(hidden, down_weight[0], preferred_element_type=F32).astype(BF16)
    mixed = pl.pallas_call(
        functools.partial(back, n_aa, n_ba),
        out_shape=jax.ShapeDtypeStruct((toks, width), BF16),
        in_specs=[vmem] * 4,
        out_specs=vmem,
        scratch_shapes=[
            pltpu.VMEM((nx, n_ba, CAP, width), BF16),
            pltpu.VMEM((max(nx - 1, 1), n_ba, CAP, width), BF16),
            pltpu.VMEM((max(nx - 1, 1), n_ba, CAP, width), BF16),
            pltpu.VMEM((n_ba, CAP, width), F32),
            pltpu.VMEM((n_ba - 1, CAP, width), BF16),
            pltpu.VMEM((n_ba, CAP, width), BF16),
        ]
        + sems(n_ba * nx)
        + sems(n_ba * (nx - 1))
        + sems(n_ba - 1),
        compiler_params=pltpu.CompilerParams(
            collective_id=1, has_side_effects=True, vmem_limit_bytes=56 * 2**20
        ),
        name="back",
    )(idx, residual, logits, partial_value.reshape(n_ba, CAP, model_width))
    return (mixed, load[0, : held // ADAPTER_RANK])


def solution(mesh):
    in_specs = (
        P("ba", None),
        P("ba", None),
        P(None, "aa"),
        P("aa", None),
        P(),
        P(),
        P("ba"),
        P("ba", None),
        P("ba", None, "aa"),
        P("ba", None, "aa"),
        P("ba", "aa", None),
    )
    out_specs = (P("ba", "aa"), P("aa"))
    return jax.shard_map(shards, mesh=mesh, in_specs=in_specs, out_specs=out_specs, check_vma=False)
```

profile of v0, /device:TPU:0, one launch (start us, length us, event | category | flops | bytes accessed | tf_op | source)
XLA Modules:
  0.0 160.8 jit_solution(10115536351519696991)
XLA Ops:
  0.6 0.7 pad_add_fusion
  1.3 0.1 copy.18.idx_ref
  1.4 0.0 copy-start.4
  1.5 1.3 copy.17.router_ref
  2.8 0.0 copy-start
  2.8 1.2 copy-done
  4.0 0.0 copy-start.1
  4.0 1.2 copy-done.1
  5.3 0.0 copy-start.2
  5.3 1.2 copy-done.2
  6.5 0.0 copy-start.3
  6.5 1.2 copy-done.3
  7.7 0.0 copy-start.7
  7.7 0.7 copy-done.7
  8.4 0.0 copy-start.8
  8.4 0.7 copy-done.8
  9.1 54.0 %front.1 = (bf16[8,48,4096]{2,1,0:T(8,128)(2,1)}, f32[128,1024]{1,0:T(8,128)S(1)}, f32[128,8]{1,0:T(8,128)S(1)}, f32[8,128]{1,0:T(8,128)S(1)}) custom-call(s32[128,3]{1,0:T(8,128)S(1)} %copy.18.idx_ref, s32[2,128]{1,0:T(2,128)S(1)} %bitcast.35, bf16[128,4096]{1,0:T(8,128)(2,1)S(1)} %copy-done, bf16[128,4096]{1,0:T(8,128)(2,1)S(1)} %copy-done.1, ...), custom_call_target="tpu_custom_call" | custom-call | tf_op jit(solution)/shard_map/front/pallas_call | solution.py:298
  63.1 0.0 copy-start.5
  63.1 0.8 copy-done.5
  63.9 0.0 copy-start.6
  63.9 0.6 copy-done.6
  64.6 0.5 slice_bitcast_fusion
  65.1 0.0 copy-start.9
  65.1 23.5 %fusion.4 = f32[384,3584]{1,0:T(8,128)} fusion(bf16[384,4096]{1,0:T(8,128)(2,1)} %bitcast.38, bf16[1,4096,3584]{2,1,0:T(8,128)(2,1)} %param.19), kind=kOutput, calls=%fused_computation.4 | convolution fusion | flops 11274289152 | bytes 38010880 | tf_op jit(solution)/shard_map/dot_general | solution.py:330
  88.6 0.0 copy-done.4
  88.6 0.0 copy-done.9
  88.6 18.0 %fusion.12.clone.4 = bf16[384,3584]{1,0:T(8,128)(2,1)S(1)} fusion(bf16[384,4096]{1,0:T(8,128)(2,1)S(1)} %bitcast.39, bf16[1,4096,3584]{2,1,0:T(8,128)(2,1)} %param.20, f32[384,3584]{1,0:T(8,128)} %fusion.4), kind=kOutput, calls=%fused_computation.8.clone.clone.clone.1 | convolution fusion | flops 11282546688 | bytes 40763392 | tf_op jit(solution)/shard_map/dot_general | solution.py:331
  106.7 18.2 %fusion.9 = bf16[384,4096]{1,0:T(8,128)(2,1)} fusion(bf16[1,3584,4096]{2,1,0:T(8,128)(2,1)} %param.21, bf16[384,3584]{1,0:T(8,128)(2,1)S(1)} %fusion.12.clone.4), kind=kOutput, calls=%fused_computation.7 | convolution fusion | flops 11275862016 | bytes 35258368 | tf_op jit(solution)/shard_map/dot_general | solution.py:333
  124.9 34.2 %back.1 = bf16[128,1024]{1,0:T(8,128)(2,1)} custom-call(s32[128,3]{1,0:T(8,128)} %copy-done.4, f32[128,1024]{1,0:T(8,128)} %copy-done.5, f32[128,8]{1,0:T(8,128)} %copy-done.6, bf16[8,48,4096]{2,1,0:T(8,128)(2,1)} %bitcast.36), custom_call_target="tpu_custom_call" | custom-call | tf_op jit(solution)/shard_map/back/pallas_call | solution.py:334
  159.1 1.7 %copy.20 = bf16[128,1024]{1,0:T(8,128)(2,1)} copy(bf16[128,1024]{1,0:T(8,128)(2,1)} %back.1) | data formatting | bytes 524288
Async XLA Ops:
  1.4 87.2 %copy-start.4 = (s32[128,3]{1,0:T(8,128)}, s32[128,3]{1,0:T(8,128)S(1)}, u32[]{:S(2)}) copy-start(s32[128,3]{1,0:T(8,128)S(1)} %copy.18.idx_ref) | copy-start | bytes 4612
  2.8 1.2 copy-start
  4.0 1.2 copy-start.1
  5.3 1.2 copy-start.2
  6.5 1.2 copy-start.3
  7.7 0.7 copy-start.7
  8.4 0.7 copy-start.8
  63.1 0.9 copy-start.5
  63.9 0.6 copy-start.6
  65.1 23.6 %copy-start.9 = (bf16[8,48,4096]{2,1,0:T(8,128)(2,1)S(1)}, bf16[8,48,4096]{2,1,0:T(8,128)(2,1)}, u32[]{:S(2)}) copy-start(bf16[8,48,4096]{2,1,0:T(8,128)(2,1)} %get-tuple-element.8) | copy-start | bytes 9437188
where the time goes:
time: 161 us
  Pallas kernels  88.1 us (55%)
  matrix products  59.8 us (37%)
  local copies, waits for them, and re-layouts  11.4 us (7%)
    pallas_call x1, Pallas kernels, shards(): pl.pallas_call(functools.partial(front, n_aa, n_ba, model_width), out_sha...  54 us
    pallas_call x1, Pallas kernels, shards(): pl.pallas_call(functools.partial(back, n_aa, n_ba), out_shape=jax.ShapeDt...  34.2 us
    dot_general x1, matrix products, shards(): gate_proj = jnp.dot(rows, gate_weight[0], preferred_element_type=F32)  23.5 us
    dot_general x1, matrix products, shards(): jnp.dot(hidden, down_weight[0], preferred_element_type=F32).astype(BF16)  18.2 us
    dot_general x1, matrix products, shards(): up_proj = jnp.dot(rows, up_weight[0], preferred_element_type=F32)  18 us
    unnamed x22, local copies, waits for them, and re-layouts  10.8 us

commit v1 on v0

v1 whole, which is shorter than its diff:
```python
import functools

import jax
import jax.numpy as jnp
from jax import lax
from jax.experimental import pallas as pl
from jax.experimental.pallas import tpu as pltpu
from jax.sharding import PartitionSpec as P

E = 8
ADAPTER_RANK = 16
CAP = 48
CORES = 2
HALVES = 2

EPS = 1e-05
ADAPTER_SCALE = 2.0
GU_SLOTS = 3
DN_SLOTS = 2
MESH = pl.DeviceIdType.MESH
F32 = jnp.float32
BF16 = jnp.bfloat16
NT = (((1,), (1,)), ((), ()))


def cols(start, width):
    return pl.ds(pl.multiple_of(start, 128), width)


def remote(src, dst, sems, i, place):
    return pltpu.make_async_remote_copy(
        src_ref=src,
        dst_ref=dst,
        send_sem=sems[0].at[i],
        recv_sem=sems[1].at[i],
        device_id=place,
        device_id_type=MESH,
    )


def layer(
    n_aa, n_ba, nt,
    head_hbm, stream_hbm, down_hbm, up_hbm, gain_hbm, router_hbm, adapter_hbm, expert_hbm,
    gate_hbm, upw_hbm, dn_hbm,
    out_ref, load_ref,
    head, stream, down, up, gain, router, adapter, expert,
    up_all, low_all, sq_all, lg_all, ld_all, res, outgoing,
    x_all, gacc, uacc, hidden, gw, uw, dw,
    ys, c1, yown, xs, c2, bs, ret,
    in_s, gu_s, dn_s,
    up_s, up_r, low_s, low_r, sq_s, sq_r, lg_s, lg_r, ld_s, ld_r,
    z_s, z_r, x_s, x_r, c_s, c_r, f_s, f_r,
    p_s, p_r, q_s, q_r, b_s, b_r,
):
    aa, ba = lax.axis_index("aa"), lax.axis_index("ba")
    nx = n_aa // CORES
    x, core = aa // CORES, lax.rem(aa, CORES)
    partner = {"aa": x * CORES + 1 - core}
    toks = head.shape[0]
    held = down.shape[1]
    model_width = head.shape[1]
    width = model_width // n_aa
    half = width // HALVES
    ff = hidden.shape[1]
    ft = ff // nt
    rows = n_ba * CAP
    split = n_ba // E
    mine = cols(aa * width, width)
    lane = cols(core * half, half)
    aa_peers = [{"aa": lax.rem(aa + k, n_aa)} for k in range(1, n_aa)]
    ba_peers = [{"ba": lax.rem(ba + k, n_ba)} for k in range(1, n_ba)]
    x_peers = [{"aa": lax.rem(x + kx, nx) * CORES + core} for kx in range(1, nx)]
    sources = [lax.rem(ba - k + n_ba, n_ba) for k in range(n_ba)]
    targets = [lax.rem(ba + k, n_ba) for k in range(n_ba)]
    origins = [lax.rem(x - kx + nx, nx) for kx in range(nx)]

    barrier = pltpu.get_barrier_semaphore()
    greeted = aa_peers + ba_peers
    for place in greeted:
        pl.semaphore_signal(barrier, inc=1, device_id=place, device_id_type=MESH)

    pairs = [
        (up_hbm, up), (head_hbm, head), (down_hbm, down), (adapter_hbm, adapter),
        (expert_hbm, expert), (stream_hbm.at[:, mine], stream), (gain_hbm.at[:, mine], gain),
        (router_hbm.at[:, mine], router),
    ]
    loads = [pltpu.make_async_copy(src, dst, in_s.at[i]) for i, (src, dst) in enumerate(pairs)]
    for copy in loads:
        copy.start()

    iterations = HALVES * nx * nt

    def gu_copies(it):
        slot = lax.rem(it, GU_SLOTS)
        t, group = lax.rem(it, nt), lax.div(it, nt)
        h, kx = lax.div(group, nx), lax.rem(group, nx)
        block = lax.rem(x - kx + nx, nx)
        copies = []
        for c in range(CORES):
            top = pl.multiple_of((block * CORES + c) * width + h * half, half)
            for j, (src, dst) in enumerate(((gate_hbm, gw), (upw_hbm, uw))):
                copies.append(pltpu.make_async_copy(
                    src.at[0, pl.ds(top, half), cols(t * ft, ft)],
                    dst.at[slot, pl.ds(c * half, half), :],
                    gu_s.at[slot, c * 2 + j],
                ))
        return copies

    far_first = list(range(1, nx)) + [0]
    chunks = [(h, kx, side) for h in range(HALVES) for kx in far_first for side in (1, 0)]

    def dn_copy(d):
        h, kx, side = chunks[d]
        block = lax.rem(x + kx, nx) * CORES + (1 - core if side else core)
        slot = d % DN_SLOTS
        return pltpu.make_async_copy(
            dn_hbm.at[0, :, cols(block * width + h * half, half)], dw.at[slot], dn_s.at[slot]
        )

    pl.semaphore_wait(barrier, len(greeted))
    loads[0].wait()
    up_copies = []
    for k in range(1, n_aa):
        to = lax.rem(aa + k, n_aa)
        up_copies.append(remote(
            up.at[:, cols(to * width, width)], up_all.at[aa], (up_s, up_r), k - 1, {"aa": to}
        ))
    for copy in up_copies:
        copy.start()
    for copy in loads[1:4]:
        copy.wait()

    eye = (
        lax.broadcasted_iota(jnp.int32, (toks, toks), 0)
        == lax.broadcasted_iota(jnp.int32, (toks, toks), 1)
    )

    def column(row):
        return jnp.sum(jnp.where(eye, jnp.broadcast_to(row, (toks, toks)), 0.0), axis=1, keepdims=True)

    def as_row(col):
        return jnp.sum(jnp.where(eye, jnp.broadcast_to(col, (toks, toks)), 0.0), axis=0, keepdims=True)

    owner = column(adapter[...].astype(F32)).astype(jnp.int32)
    local = owner - aa * (held // ADAPTER_RANK)
    lanes = lax.broadcasted_iota(jnp.int32, (toks, held), 1)
    projected = jnp.dot(head[...], down[...], preferred_element_type=F32)
    low_all[aa] = jnp.where(local == lanes // ADAPTER_RANK, projected, 0.0).astype(BF16)
    low_copies = [
        remote(low_all.at[aa], low_all.at[aa], (low_s, low_r), i, p) for i, p in enumerate(aa_peers)
    ]
    for copy in low_copies:
        copy.start()
    tally = jnp.sum((local == lanes).astype(F32), axis=0, keepdims=True)
    ld_all[ba] = jnp.broadcast_to(tally, ld_all.shape[1:])
    ld_copies = [
        remote(ld_all.at[ba], ld_all.at[ba], (ld_s, ld_r), i, p) for i, p in enumerate(ba_peers)
    ]
    for copy in ld_copies:
        copy.start()
    for copy in loads[4:]:
        copy.wait()
    for it in range(min(GU_SLOTS, iterations)):
        for copy in gu_copies(it):
            copy.start()
    for d in range(DN_SLOTS):
        dn_copy(d).start()

    up_all[aa] = up[:, mine]
    gacc[...] = jnp.zeros(gacc.shape, F32)
    uacc[...] = jnp.zeros(uacc.shape, F32)
    first, second = expert[0:1, :], expert[1:2, :]
    experts = lax.broadcasted_iota(jnp.int32, (E, toks), 0)
    hit0, hit1 = (first == experts).astype(F32), (second == experts).astype(F32)
    hits = hit0 + hit1
    earlier = (
        lax.broadcasted_iota(jnp.int32, (toks, toks), 0)
        < lax.broadcasted_iota(jnp.int32, (toks, toks), 1)
    ).astype(F32)
    place = jnp.dot(hits.astype(BF16), earlier.astype(BF16), preferred_element_type=F32)
    marked = jnp.where(hits > 0.0, place, -1.0).astype(jnp.int32)
    spots = lax.broadcasted_iota(jnp.int32, (CAP, toks), 0)
    picks = jnp.concatenate(
        [(marked[e : e + 1, :] == spots).astype(F32).astype(BF16) for e in range(E)], axis=0
    )

    for copy in low_copies + up_copies:
        copy.wait_recv()
    delta = jnp.dot(low_all[0], up_all[0], preferred_element_type=F32)
    for j in range(1, n_aa):
        delta = delta + jnp.dot(low_all[j], up_all[j], preferred_element_type=F32)
    res[...] = stream[...].astype(F32) + ADAPTER_SCALE * delta
    square = as_row(jnp.sum(res[...] * res[...], axis=1, keepdims=True))
    sq_all[aa] = jnp.broadcast_to(square, sq_all.shape[1:])
    sq_copies = [
        remote(sq_all.at[aa], sq_all.at[aa], (sq_s, sq_r), i, p) for i, p in enumerate(aa_peers)
    ]
    for copy in sq_copies:
        copy.start()
    for copy in sq_copies:
        copy.wait_recv()
    total = sq_all[0]
    for j in range(1, n_aa):
        total = total + sq_all[j]
    inv_norm = column(lax.rsqrt(total[0:1, :] / model_width + EPS))
    normed = (res[...] * inv_norm * gain[...]).astype(BF16)

    def here(h, block):
        return h * nx + block

    def dispatch(h, k):
        return remote(
            outgoing.at[h, lax.div(targets[k], split)], x_all.at[here(h, x), ba, :, lane],
            (z_s, z_r), h * (n_ba - 1) + k - 1, {"ba": targets[k]},
        )

    for h in range(HALVES):
        sent = jnp.dot(picks, normed[:, h * half : (h + 1) * half], preferred_element_type=F32)
        outgoing[h] = sent.astype(BF16).reshape(E, CAP, half)
        for k in range(1, n_ba):
            dispatch(h, k).start()
        x_all[here(h, x), ba, :, lane] = outgoing[h, lax.div(ba, split)]

    lg_all[aa] = lax.dot_general(router[...], normed, NT, preferred_element_type=F32)
    lg_copies = [
        remote(lg_all.at[aa], lg_all.at[aa], (lg_s, lg_r), i, p) for i, p in enumerate(aa_peers)
    ]
    for copy in lg_copies:
        copy.start()

    def across(h, k, kx):
        block = x_all.at[here(h, x), sources[k], :, lane]
        i = (h * n_ba + k) * (nx - 1) + kx - 1
        return remote(block, block, (x_s, x_r), i, x_peers[kx - 1])

    def beside(h, k):
        block = x_all.at[here(h, x), sources[k], :, lane]
        return remote(block, block, (c_s, c_r), h * n_ba + k, partner)

    def passed(h, kx):
        block = x_all.at[here(h, origins[kx]), :, :, lane]
        return remote(block, block, (f_s, f_r), h * (nx - 1) + kx - 1, partner)

    def forward(h, k):
        if k:
            dispatch(h, k).wait_recv()
        for kx in range(1, nx):
            across(h, k, kx).start()
        beside(h, k).start()

    def settle(h):
        for k in range(n_ba):
            beside(h, k).wait_recv()

    def collect(h, kx):
        for k in range(n_ba):
            across(h, k, kx).wait_recv()
        passed(h, kx).start()

    per_half = nx * nt
    hooks = {}

    def hook(it, fn, *args):
        hooks.setdefault(it, []).append(functools.partial(fn, *args))

    for kx in range(1, nx):
        hook(max(1, kx * nt - 1), collect, 0, kx)
        hook(kx * nt, lambda kx: passed(0, kx).wait_recv(), kx)
    for k in range(n_ba):
        at = 1 + (0 if k < n_ba // 2 else (1 if k < 3 * n_ba // 4 else 2))
        hook(min(at, per_half - 1), forward, 1, k)
    hook(per_half, settle, 1)
    for kx in range(1, nx):
        hook(per_half + max(1, kx * nt - 1), collect, 1, kx)
        hook(per_half + kx * nt, lambda kx: passed(1, kx).wait_recv(), kx)

    def step(it, finish):
        for at, fns in hooks.items():
            if (at >= iterations - nt) == finish:
                @pl.when(it == at)
                def _():
                    for fn in fns:
                        fn()
        for copy in gu_copies(it):
            copy.wait()
        slot = lax.rem(it, GU_SLOTS)
        t, group = lax.rem(it, nt), lax.div(it, nt)
        h, kx = lax.div(group, nx), lax.rem(group, nx)
        lhs = x_all[here(h, lax.rem(x - kx + nx, nx))].reshape(rows, CORES * half)
        g = gacc[t] + jnp.dot(lhs, gw[slot], preferred_element_type=F32)
        u = uacc[t] + jnp.dot(lhs, uw[slot], preferred_element_type=F32)
        if finish:
            hidden[:, cols(t * ft, ft)] = (g / (1.0 + jnp.exp(-g)) * u).astype(BF16)
        else:
            gacc[t] = g
            uacc[t] = u

            @pl.when(it + GU_SLOTS < iterations)
            def _():
                for copy in gu_copies(it + GU_SLOTS):
                    copy.start()

    for k in range(n_ba):
        forward(0, k)
    settle(0)

    @pl.loop(0, iterations - nt)
    def _(it):
        step(it, False)

    @pl.loop(iterations - nt, iterations)
    def _(it):
        step(it, True)

    order = list(range(1, n_ba)) + [0]

    def to_partner(h, kx):
        return remote(ys.at[h, kx], c1.at[h, kx], (p_s, p_r), h * nx + kx, partner)

    def to_chip(h, kx, k):
        i = (h * (nx - 1) + kx - 1) * n_ba + k
        return remote(
            xs.at[h, kx - 1, targets[k]], c2.at[h, kx - 1, targets[k]], (q_s, q_r), i, x_peers[kx - 1]
        )

    def home(h, k):
        return remote(
            bs.at[h, k - 1], ret.at[h, ba], (b_s, b_r), h * (n_ba - 1) + k - 1, {"ba": targets[k]}
        )

    def give(h, k):
        to = targets[k]
        whole = yown[h, to]
        for kx in range(1, nx):
            to_chip(h, kx, k).wait_recv()
            whole = whole + c2[h, kx - 1, to].astype(F32)
        if k:
            bs[h, k - 1] = whole.astype(BF16)
            home(h, k).start()
        else:
            ret[h, ba] = whole.astype(BF16)

    gives = {}
    last = len(chunks) - 1
    ready = len(chunks) // HALVES - 1
    for n, k in enumerate(order):
        at = ready + (0, 0, 1, 2, 2, 3, 3, 4)[n * 8 // n_ba]
        gives.setdefault(min(at, last), []).append((0, k))
    for k in order:
        gives.setdefault(last, []).append((1, k))

    for d, (h, kx, side) in enumerate(chunks):
        dn_copy(d).wait()
        y = jnp.dot(hidden[...], dw[d % DN_SLOTS], preferred_element_type=F32)
        if side:
            ys[h, kx] = y.astype(BF16).reshape(n_ba, CAP, half)
            to_partner(h, kx).start()
        else:
            yown[h] = y.reshape(n_ba, CAP, half)
            to_partner(h, kx).wait_recv()
            if kx:
                for k in order:
                    to = targets[k]
                    xs[h, kx - 1, to] = (yown[h, to] + c1[h, kx, to].astype(F32)).astype(BF16)
                    to_chip(h, kx, k).start()
            else:
                yown[h] = yown[h] + c1[h, kx].astype(F32)
        if d + DN_SLOTS < len(chunks):
            dn_copy(d + DN_SLOTS).start()
        for hh, k in gives.get(d, []):
            give(hh, k)

    for copy in lg_copies + ld_copies:
        copy.wait_recv()
    logits = lg_all[0]
    for j in range(1, n_aa):
        logits = logits + lg_all[j]
    load = ld_all[0]
    for j in range(1, n_ba):
        load = load + ld_all[j]
    load_ref[...] = load
    own0 = jnp.sum(hit0 * logits, axis=0, keepdims=True)
    own1 = jnp.sum(hit1 * logits, axis=0, keepdims=True)
    weight0 = column(1.0 / (1.0 + jnp.exp(own1 - own0)))
    weight1 = column(1.0 / (1.0 + jnp.exp(own0 - own1)))
    seats = lax.broadcasted_iota(jnp.int32, (toks, rows), 1)

    def picked(which, hit):
        seat = which.astype(F32) * (split * CAP) + jnp.sum(hit * place, axis=0, keepdims=True)
        seat = column(seat).astype(jnp.int32)
        found = seats == seat
        for j in range(1, split):
            found = found | (seats == seat + j * CAP)
        return found.astype(F32).astype(BF16)

    pick0, pick1 = picked(first, hit0), picked(second, hit1)
    for h in range(HALVES):
        for k in range(1, n_ba):
            home(h, k).wait_recv()
        part = slice(h * half, (h + 1) * half)
        back = ret[h].reshape(rows, half)
        mixed = weight0 * jnp.dot(pick0, back, preferred_element_type=F32)
        mixed = mixed + weight1 * jnp.dot(pick1, back, preferred_element_type=F32)
        out_ref[:, part] = (res[:, part] + mixed).astype(BF16)

    for copy in up_copies + low_copies + sq_copies + lg_copies + ld_copies:
        copy.wait_send()
    for h in range(HALVES):
        for k in range(n_ba):
            if k:
                dispatch(h, k).wait_send()
                home(h, k).wait_send()
            beside(h, k).wait_send()
            for kx in range(1, nx):
                across(h, k, kx).wait_send()
                to_chip(h, kx, k).wait_send()
        for kx in range(nx):
            if kx:
                passed(h, kx).wait_send()
            to_partner(h, kx).wait_send()


def shards(
    head_outputs,
    stream,
    adapter_down_factors,
    adapter_up_factors,
    norm_gain_vector,
    router_matrix,
    token_adapter_index,
    token_expert_index,
    gate_weight,
    up_weight,
    down_weight,
):
    toks, model_width = head_outputs.shape
    n_aa, n_ba = lax.axis_size("aa"), lax.axis_size("ba")
    nx = n_aa // CORES
    held = adapter_down_factors.shape[1]
    ff = gate_weight.shape[2]
    width = model_width // n_aa
    half = width // HALVES
    rows = n_ba * CAP
    nt = 2 if ff % 512 == 0 else 1
    dma = pltpu.SemaphoreType.DMA
    vmem = pltpu.VMEM
    far = max(nx - 1, 1)

    def sems(n):
        return [dma((max(n, 1),)), dma((max(n, 1),))]

    mixed, load = pl.pallas_call(
        functools.partial(layer, n_aa, n_ba, nt),
        out_shape=(
            jax.ShapeDtypeStruct((toks, width), BF16),
            jax.ShapeDtypeStruct((8, held), F32),
        ),
        in_specs=[pl.BlockSpec(memory_space=pl.ANY)] * 11,
        out_specs=(pl.BlockSpec(memory_space=pltpu.VMEM),) * 2,
        scratch_shapes=[
            vmem((toks, model_width), BF16),
            vmem((toks, width), BF16),
            vmem((model_width, held), BF16),
            vmem((held, model_width), BF16),
            vmem((1, width), F32),
            vmem((E, width), BF16),
            vmem((1, toks), jnp.int32),
            vmem((2, toks), jnp.int32),
            vmem((n_aa, held, width), BF16),
            vmem((n_aa, toks, held), BF16),
            vmem((n_aa, 8, toks), F32),
            vmem((n_aa, E, toks), F32),
            vmem((n_ba, 8, held), F32),
            vmem((toks, width), F32),
            vmem((HALVES, E, CAP, half), BF16),
            vmem((HALVES * nx, n_ba, CAP, CORES * half), BF16),
            vmem((nt, rows, ff // nt), F32),
            vmem((nt, rows, ff // nt), F32),
            vmem((rows, ff), BF16),
            vmem((GU_SLOTS, CORES * half, ff // nt), BF16),
            vmem((GU_SLOTS, CORES * half, ff // nt), BF16),
            vmem((DN_SLOTS, ff, half), BF16),
            vmem((HALVES, nx, n_ba, CAP, half), BF16),
            vmem((HALVES, nx, n_ba, CAP, half), BF16),
            vmem((HALVES, n_ba, CAP, half), F32),
            vmem((HALVES, far, n_ba, CAP, half), BF16),
            vmem((HALVES, far, n_ba, CAP, half), BF16),
            vmem((HALVES, n_ba - 1, CAP, half), BF16),
            vmem((HALVES, n_ba, CAP, half), BF16),
            dma((8,)),
            dma((GU_SLOTS, 2 * CORES)),
            dma((DN_SLOTS,)),
        ]
        + sems(n_aa - 1) * 4
        + sems(n_ba - 1)
        + sems(HALVES * (n_ba - 1))
        + sems(HALVES * n_ba * (nx - 1))
        + sems(HALVES * n_ba)
        + sems(HALVES * (nx - 1))
        + sems(HALVES * nx)
        + sems(HALVES * n_ba * (nx - 1))
        + sems(HALVES * (n_ba - 1)),
        compiler_params=pltpu.CompilerParams(
            collective_id=0, has_side_effects=True, vmem_limit_bytes=67043328
        ),
        name="layer",
    )(
        head_outputs, stream, adapter_down_factors, adapter_up_factors,
        norm_gain_vector[None, :], router_matrix.T, token_adapter_index[None, :],
        token_expert_index.T, gate_weight, up_weight, down_weight,
    )
    return (mixed, load[0, : held // ADAPTER_RANK])


def solution(mesh):
    in_specs = (
        P("ba", None),
        P("ba", None),
        P(None, "aa"),
        P("aa", None),
        P(),
        P(),
        P("ba"),
        P("ba", None),
        P("ba", None, "aa"),
        P("ba", None, "aa"),
        P("ba", "aa", None),
    )
    out_specs = (P("ba", "aa"), P("aa"))
    return jax.shard_map(shards, mesh=mesh, in_specs=in_specs, out_specs=out_specs, check_vma=False)
```

time: 161 us -> 96.6 us (0.60)
  matrix products: 59.8 us -> 0 us
  local copies, waits for them, and re-layouts: 11.4 us -> 2.86 us
  Pallas kernels: 88.1 us -> 92.4 us
    dot_general x3 -> x0, matrix products: 59.8 us -> none  [the longest x1 23.5 us: shards(): gate_proj = jnp.dot(rows, gate_weight[0], preferred_element_type=F32)]
    unnamed x22 -> x1, local copies, waits for them, and re-layouts: 10.8 us -> 1.67 us
    pallas_call x2 -> x1, Pallas kernels: 88.1 us -> 92.4 us  [shards(): pl.pallas_call(functools.partial(layer, n_aa, n_ba, nt), out_shape=(jax.S...]
where the time goes in v1:
time: 96.6 us; the launch traced here: 95.9 us
  Pallas kernels  92.4 us (96%)
  local copies, waits for them, and re-layouts  2.86 us (3%)
    pallas_call x1, Pallas kernels, shards(): pl.pallas_call(functools.partial(layer, n_aa, n_ba, nt), out_shape=(jax.S...  92.4 us

profile of v1, /device:TPU:0, one launch (start us, length us, event | category | flops | bytes accessed | tf_op | source)
XLA Modules:
  0.0 95.9 jit_solution(3733312267936367868)
XLA Ops:
  0.6 92.4 %layer.1 = (bf16[128,1024]{1,0:T(8,128)(2,1)}, f32[8,128]{1,0:T(8,128)}) custom-call(bf16[128,4096]{1,0:T(8,128)(2,1)} %head_hbm.1, bf16[128,4096]{1,0:T(8,128)(2,1)} %stream_hbm.1, bf16[4096,128]{1,0:T(8,128)(2,1)} %down_hbm.1, bf16[128,4096]{1,0:T(8,128)(2,1)} %up_hbm.1, f32[1,4096]{1,0:T(1,128)} %bitcast.7, bf16[8,4096]{1,0:T(8,128)(2,1)} %bitcast.6, ...), custom_call_target="tpu_custom_call" | custom-call | tf_op jit(solution)/shard_map/layer/pallas_call | solution.py:452
  93.0 1.2 %slice_bitcast_fusion = f32[8]{0:T(128)} fusion(f32[8,128]{1,0:T(8,128)} %get-tuple-element.5), kind=kLoop, calls=%fused_computation | loop fusion | bytes 64 | tf_op jit(solution)/shard_map/squeeze | solution.py:512
  94.2 1.7 %copy.14 = bf16[128,1024]{1,0:T(8,128)(2,1)} copy(bf16[128,1024]{1,0:T(8,128)(2,1)} %get-tuple-element.8) | data formatting | bytes 524288

commit v2 on v1

v2 whole, which is shorter than its diff:
```python
import functools

import jax
import jax.numpy as jnp
from jax import lax
from jax.experimental import pallas as pl
from jax.experimental.pallas import tpu as pltpu
from jax.sharding import PartitionSpec as P

E = 8
ADAPTER_RANK = 16
CAP = 48
CORES = 2
PARTS = 4

EPS = 1e-05
ADAPTER_SCALE = 2.0
GU_DEPTH = 3
DN_SLOTS = 2
MESH = pl.DeviceIdType.MESH
F32 = jnp.float32
BF16 = jnp.bfloat16
NT = (((1,), (1,)), ((), ()))


def cols(start, width):
    return pl.ds(pl.multiple_of(start, 128), width)


def remote(src, dst, sems, i, place):
    return pltpu.make_async_remote_copy(
        src_ref=src,
        dst_ref=dst,
        send_sem=sems[0].at[0],
        recv_sem=sems[1].at[i],
        device_id=place,
        device_id_type=MESH,
    )


def layer(
    n_aa, n_ba, nt,
    head_hbm, stream_hbm, down_hbm, up_hbm, gain_hbm, router_hbm, adapter_hbm, expert_hbm,
    gate_hbm, upw_hbm, dn_hbm,
    out_hbm, load_ref,
    head, stream, down, up, gain, router, adapter, expert,
    d_send, d_recv, e_send, e_recv, stat_all, note_all, ld_all, res, outgoing, scale,
    pick0, pick1, weight0, weight1, out,
    x_all, gacc, uacc, hidden, gw, uw, dw,
    ys, c1, yown, yfar, xs, c2, bs, ret,
    in_s, gu_s, dn_s, out_s,
    d_s, d_r, e_s, e_r, stat_s, stat_r, note_s, note_r, ld_s, ld_r,
    z_s, z_r, x_s, x_r, c_s, c_r, f_s, f_r,
    p_s, p_r, q_s, q_r, b_s, b_r,
):
    aa, ba = lax.axis_index("aa"), lax.axis_index("ba")
    nx = n_aa // CORES
    x, core = aa // CORES, lax.rem(aa, CORES)
    partner = {"aa": x * CORES + 1 - core}
    toks = head.shape[0]
    held = down.shape[1]
    model_width = head.shape[1]
    width = model_width // n_aa
    part = width // PARTS
    ff = hidden.shape[1]
    ft = ff // nt
    rows = n_ba * CAP
    split = n_ba // E
    mine = cols(aa * width, width)
    lane = cols(core * part, part)
    aa_peers = [{"aa": lax.rem(aa + k, n_aa)} for k in range(1, n_aa)]
    ba_peers = [{"ba": lax.rem(ba + k, n_ba)} for k in range(1, n_ba)]
    x_peers = [{"aa": lax.rem(x + kx, nx) * CORES + core} for kx in range(1, nx)]
    sources = [lax.rem(ba - k + n_ba, n_ba) for k in range(n_ba)]
    targets = [lax.rem(ba + k, n_ba) for k in range(n_ba)]
    origins = [lax.rem(x - kx + nx, nx) for kx in range(nx)]
    ahead = [lax.rem(x + kx, nx) for kx in range(nx)]
    far = list(range(1, nx))
    far_first = far + [0]

    barrier = pltpu.get_barrier_semaphore()
    greeted = aa_peers + ba_peers
    for place in greeted:
        pl.semaphore_signal(barrier, inc=1, device_id=place, device_id_type=MESH)

    pairs = [
        (head_hbm, head), (down_hbm, down), (adapter_hbm, adapter), (up_hbm, up),
        (expert_hbm, expert), (stream_hbm.at[:, mine], stream), (gain_hbm.at[:, mine], gain),
        (router_hbm.at[:, mine], router),
    ]
    loads = [pltpu.make_async_copy(src, dst, in_s.at[i]) for i, (src, dst) in enumerate(pairs)]
    for copy in loads:
        copy.start()

    groups = [(0, kx) for kx in range(nx)]
    for q in range(1, PARTS):
        groups += [(q, 0)] + ([(q - 1, kx) for kx in far] if q > 1 else [])
    groups += [(PARTS - 1, kx) for kx in far] if PARTS > 1 else []

    def gu_copies(n, t):
        q, kx = groups[n]
        slot = (n % GU_DEPTH) * nt + t
        copies = []
        for c in range(CORES):
            top = pl.multiple_of((origins[kx] * CORES + c) * width + q * part, part)
            for j, (src, dst) in enumerate(((gate_hbm, gw), (upw_hbm, uw))):
                copies.append(pltpu.make_async_copy(
                    src.at[0, pl.ds(top, part), cols(t * ft, ft)],
                    dst.at[slot, pl.ds(c * part, part), :],
                    gu_s.at[slot, j],
                ))
        return copies

    chunks = [(q, kx) for q in range(PARTS) for kx in far_first]

    def dn_copies(d):
        q, kx = chunks[d]
        slot = d % DN_SLOTS
        copies = []
        for side in range(CORES):
            block = ahead[kx] * CORES + (1 - core if side else core)
            copies.append(pltpu.make_async_copy(
                dn_hbm.at[0, :, cols(block * width + q * part, part)],
                dw.at[slot, side],
                dn_s.at[slot, side],
            ))
        return copies

    eye = (
        lax.broadcasted_iota(jnp.int32, (toks, toks), 0)
        == lax.broadcasted_iota(jnp.int32, (toks, toks), 1)
    )

    def column(row):
        return jnp.sum(jnp.where(eye, jnp.broadcast_to(row, (toks, toks)), 0.0), axis=1, keepdims=True)

    def as_row(col):
        return jnp.sum(jnp.where(eye, jnp.broadcast_to(col, (toks, toks)), 0.0), axis=0, keepdims=True)

    for copy in loads[:3]:
        copy.wait()
    owner = column(adapter[...].astype(F32)).astype(jnp.int32)
    local = owner - aa * (held // ADAPTER_RANK)
    lanes = lax.broadcasted_iota(jnp.int32, (toks, held), 1)
    projected = jnp.dot(head[...], down[...], preferred_element_type=F32)
    low = jnp.where(local == lanes // ADAPTER_RANK, projected, 0.0).astype(BF16)
    tally = jnp.sum((local == lanes).astype(F32), axis=0, keepdims=True)
    ld_all[ba] = jnp.broadcast_to(tally, ld_all.shape[1:])
    loads[3].wait()

    def term(q, kx, other):
        block = ahead[kx] * CORES + (1 - core if other else core)
        return jnp.dot(low, up[:, cols(block * width + q * part, part)], preferred_element_type=F32)

    def to_side(q, kx):
        return remote(d_send.at[q, kx], d_recv.at[q, kx], (d_s, d_r), q * nx + kx, partner)

    def to_far(q, kx):
        i = q * (nx - 1) + kx - 1
        return remote(e_send.at[q, kx - 1], e_recv.at[q, kx - 1], (e_s, e_r), i, x_peers[kx - 1])

    for q in range(PARTS):
        for kx in far_first:
            d_send[q, kx] = term(q, kx, True).astype(BF16)
    pl.semaphore_wait(barrier, len(greeted))
    for q in range(PARTS):
        for kx in far_first:
            to_side(q, kx).start()
    for copy in loads[4:]:
        copy.wait()
    for n in range(min(GU_DEPTH, len(groups))):
        for t in range(nt):
            for copy in gu_copies(n, t):
                copy.start()
    for d in range(DN_SLOTS):
        for copy in dn_copies(d):
            copy.start()
    ld_copies = [
        remote(ld_all.at[ba], ld_all.at[ba], (ld_s, ld_r), 0, p) for i, p in enumerate(ba_peers)
    ]
    for q in range(PARTS):
        for kx in far:
            own = term(q, kx, False)
            to_side(q, kx).wait_recv()
            e_send[q, kx - 1] = (own + d_recv[q, kx].astype(F32)).astype(BF16)
            to_far(q, kx).start()
    for copy in ld_copies:
        copy.start()

    first, second = expert[0:1, :], expert[1:2, :]
    experts = lax.broadcasted_iota(jnp.int32, (E, toks), 0)
    hit0, hit1 = (first == experts).astype(F32), (second == experts).astype(F32)
    hits = hit0 + hit1
    earlier = (
        lax.broadcasted_iota(jnp.int32, (toks, toks), 0)
        < lax.broadcasted_iota(jnp.int32, (toks, toks), 1)
    ).astype(F32)
    place = jnp.dot(hits.astype(BF16), earlier.astype(BF16), preferred_element_type=F32)
    marked = jnp.where(hits > 0.0, place, -1.0)
    spots = lax.broadcasted_iota(jnp.int32, (CAP, toks), 0)
    picks = jnp.concatenate(
        [(marked[e : e + 1, :].astype(jnp.int32) == spots).astype(F32).astype(BF16) for e in range(E)],
        axis=0,
    )
    seats = lax.broadcasted_iota(jnp.int32, (toks, rows), 1)

    def picked(which, hit):
        seat = which.astype(F32) * (split * CAP) + jnp.sum(hit * place, axis=0, keepdims=True)
        seat = column(seat).astype(jnp.int32)
        found = seats == seat
        for j in range(1, split):
            found = found | (seats == seat + j * CAP)
        return found.astype(F32).astype(BF16)

    pick0[...] = picked(first, hit0)
    pick1[...] = picked(second, hit1)

    def everyone(buf, sems):
        others = buf.at[pl.ds(0, buf.shape[0] - 1)]
        return remote(others, others, sems, 0, partner)

    def here(q, block):
        return q * nx + block

    def dispatch(q, k):
        return remote(
            outgoing.at[q, lax.div(targets[k], split)], x_all.at[here(q, x), ba, :, lane],
            (z_s, z_r), q * (n_ba - 1) + k - 1, {"ba": targets[k]},
        )

    square = jnp.zeros((toks, 1), F32)
    votes = jnp.zeros((E, toks), F32)
    for q in range(PARTS):
        where = slice(q * part, (q + 1) * part)
        delta = term(q, 0, False)
        to_side(q, 0).wait_recv()
        delta = delta + d_recv[q, 0].astype(F32)
        for kx in far:
            to_far(q, kx).wait_recv()
            delta = delta + e_recv[q, kx - 1].astype(F32)
        residual = stream[:, where].astype(F32) + ADAPTER_SCALE * delta
        res[:, where] = residual
        gained = (residual * gain[:, where]).astype(BF16)
        sent = jnp.dot(picks, gained, preferred_element_type=F32)
        outgoing[q] = sent.astype(BF16).reshape(E, CAP, part)
        for k in range(1, n_ba):
            dispatch(q, k).start()
        x_all[here(q, x), ba, :, lane] = outgoing[q, lax.div(ba, split)]
        square = square + jnp.sum(residual * residual, axis=1, keepdims=True)
        votes = votes + lax.dot_general(router[:, where], gained, NT, preferred_element_type=F32)
    stat_all[aa, 0:E] = votes
    stat_all[aa, E : 2 * E] = jnp.broadcast_to(as_row(square), (E, toks))
    stat_copies = [
        remote(stat_all.at[aa], stat_all.at[aa], (stat_s, stat_r), 0, p) for i, p in enumerate(aa_peers)
    ]
    for copy in stat_copies:
        copy.start()
    note_copies = [
        remote(note_all.at[ba], note_all.at[ba], (note_s, note_r), 0, p) for i, p in enumerate(ba_peers)
    ]

    def weigh():
        everyone(stat_all, (stat_s, stat_r)).wait_recv()
        stats = stat_all[0]
        for j in range(1, n_aa):
            stats = stats + stat_all[j]
        inv = lax.rsqrt(stats[E : 2 * E, :] / model_width + EPS)
        note_all[ba, 0:E] = marked
        note_all[ba, E : 2 * E] = inv
        for copy in note_copies:
            copy.start()
        logits = stats[0:E, :] * inv
        own0 = jnp.sum(hit0 * logits, axis=0, keepdims=True)
        own1 = jnp.sum(hit1 * logits, axis=0, keepdims=True)
        weight0[...] = jnp.broadcast_to(column(1.0 / (1.0 + jnp.exp(own1 - own0))), weight0.shape)
        weight1[...] = jnp.broadcast_to(column(1.0 / (1.0 + jnp.exp(own0 - own1))), weight1.shape)

    def read_notes():
        everyone(note_all, (note_s, note_r)).wait_recv()
        everyone(ld_all, (ld_s, ld_r)).wait_recv()
        load = ld_all[0]
        for j in range(1, n_ba):
            load = load + ld_all[j]
        load_ref[...] = load[0:1, 0 : load_ref.shape[1]]
        for s in range(n_ba):
            note = note_all[s, pl.ds(lax.div(ba, split), 1), :]
            seen = note.astype(jnp.int32) == spots
            inv = jnp.sum(jnp.where(seen, note_all[s, E : E + 1, :], 0.0), axis=1, keepdims=True)
            scale[s * CAP : (s + 1) * CAP, :] = jnp.broadcast_to(inv, (CAP, scale.shape[1]))

    def across(q, k, kx):
        block = x_all.at[here(q, x), sources[k], :, lane]
        return remote(block, block, (x_s, x_r), q * (nx - 1) + kx - 1, x_peers[kx - 1])

    def beside(q, k):
        block = x_all.at[here(q, x), sources[k], :, lane]
        return remote(block, block, (c_s, c_r), q, partner)

    def passed(q, kx):
        block = x_all.at[here(q, origins[kx]), :, :, lane]
        return remote(block, block, (f_s, f_r), q * (nx - 1) + kx - 1, partner)

    arrival = list(range(n_ba))

    def forward(q, k):
        if k:
            dispatch(q, k).wait_recv()
        for kx in far:
            across(q, k, kx).start()
        beside(q, k).start()

    def collect(q, kx):
        block = x_all.at[here(q, origins[kx]), :, :, lane]
        i = q * (nx - 1) + kx - 1
        remote(block, block, (x_s, x_r), i, x_peers[kx - 1]).wait_recv()
        passed(q, kx).start()

    steps = len(groups) * nt
    hooks = {}

    def hook(it, fn, *args):
        hooks.setdefault(min(it, steps - 1), []).append(functools.partial(fn, *args))

    def whole(it):
        return -(-it // nt) * nt if it > 3 * nt else it

    for q in range(1, PARTS):
        need = groups.index((q, 0)) * nt
        for n, k in enumerate(arrival):
            due = -(-(264 * (q - 1) + 264 * (n + 1) // n_ba + 60) // 100) * nt // 2
            hook(whole(min(max(due, 1), need)), forward, q, k)
    for q in range(PARTS):
        for kx in far:
            need = groups.index((q, kx)) * nt
            floor = groups.index((q, 0)) * nt + (1 if q == 0 else nt)
            hook(max(need - (nt if q else 1), min(floor, need)), collect, q, kx)
    hook((len(groups) - 2) * nt, read_notes)

    def ready(n):
        q, kx = groups[n]
        if kx:
            passed(q, kx).wait_recv()
        else:
            block = x_all.at[here(q, x), :, :, lane]
            remote(block, block, (c_s, c_r), q, partner).wait_recv()

    for k in arrival:
        forward(0, k)
    weigh()
    for n, (q, kx) in enumerate(groups):
        for fn in hooks.get(n * nt, []):
            fn()
        ready(n)

        def fetched(t):
            slot = (n % GU_DEPTH) * nt + t
            for j, buf in enumerate((gw, uw)):
                pltpu.make_async_copy(buf.at[slot], buf.at[slot], gu_s.at[slot, j]).wait()

        def tile(t):
            slot = (n % GU_DEPTH) * nt + t
            lhs = x_all[here(q, origins[kx])].reshape(rows, CORES * part)
            g = jnp.dot(lhs, gw[slot], preferred_element_type=F32)
            u = jnp.dot(lhs, uw[slot], preferred_element_type=F32)
            if n:
                g = gacc[t] + g
                u = uacc[t] + u
            if n == len(groups) - 1:
                factor = scale[:, 0:1]
                g = g * factor
                hidden[:, cols(t * ft, ft)] = (g / (1.0 + jnp.exp(-g)) * (u * factor)).astype(BF16)
            else:
                gacc[t] = g
                uacc[t] = u

        def refill(t):
            if n + GU_DEPTH < len(groups):
                for copy in gu_copies(n + GU_DEPTH, t):
                    copy.start()

        between = [hooks.get(n * nt + j, []) for j in range(1, nt)]
        if nt == 2 and not any(between):
            for stage in (fetched, tile, refill):
                for t in range(nt):
                    stage(t)
        else:
            @pl.loop(0, nt)
            def _(t):
                for j, fns in enumerate(between):
                    if fns:
                        @pl.when(t == j + 1)
                        def _():
                            for fn in fns:
                                fn()
                fetched(t)
                tile(t)
                refill(t)

    def to_partner(q, kx):
        return remote(ys.at[q, kx], c1.at[q, kx], (p_s, p_r), q * nx + kx, partner)

    def to_chip(q, kx, k):
        i = (q * (nx - 1) + kx - 1) * n_ba + k
        return remote(
            xs.at[q, kx - 1, targets[k]], c2.at[q, kx - 1, targets[k]], (q_s, q_r), i, x_peers[kx - 1]
        )

    def home(q, k):
        return remote(
            bs.at[q, k - 1], ret.at[q, ba], (b_s, b_r), q, {"ba": targets[k]}
        )

    def give(q, k):
        to = targets[k]
        whole = yown[q, to]
        for kx in far:
            to_chip(q, kx, k).wait_recv()
            whole = whole + c2[q, kx - 1, to].astype(F32)
        if k:
            bs[q, k - 1] = whole.astype(BF16)
            home(q, k).start()
        else:
            ret[q, ba] = whole.astype(BF16)

    def leave(q):
        where = pl.ds(q * part, part)
        return pltpu.make_async_copy(out.at[:, where], out_hbm.at[:, where], out_s.at[q])

    def blend(q):
        remote(bs.at[q], bs.at[q], (b_s, b_r), q, partner).wait_recv()
        where = slice(q * part, (q + 1) * part)
        back = ret[q].reshape(rows, part)
        mixed = weight0[:, 0:1] * jnp.dot(pick0[...], back, preferred_element_type=F32)
        mixed = mixed + weight1[:, 0:1] * jnp.dot(pick1[...], back, preferred_element_type=F32)
        out[:, where] = (res[:, where] + mixed).astype(BF16)
        leave(q).start()

    order = list(range(1, n_ba)) + [0]
    last = len(chunks) - 1
    gives = {}
    for q in range(PARTS):
        for n, k in enumerate(order):
            due = -(-(540 + 420 * q + 52 * n * 8 // n_ba) // 160) - 1
            due = max(due * nx // 2, (q + 1) * nx)
            gives.setdefault(min(due, last), []).append((q, k))

    def finish(q, kx):
        to_partner(q, kx).wait_recv()
        if kx:
            for k in order:
                to = targets[k]
                xs[q, kx - 1, to] = (yfar[kx - 1, to] + c1[q, kx, to].astype(F32)).astype(BF16)
                to_chip(q, kx, k).start()
        else:
            yown[q] = yown[q] + c1[q, kx].astype(F32)

    late = None
    for d, (q, kx) in enumerate(chunks):
        for copy in dn_copies(d):
            copy.wait()
        slot = d % DN_SLOTS
        y = [jnp.dot(hidden[...], dw[slot, i], preferred_element_type=F32) for i in range(CORES)]
        ys[q, kx] = y[1].astype(BF16).reshape(n_ba, CAP, part)
        to_partner(q, kx).start()
        if kx:
            yfar[kx - 1] = y[0].reshape(n_ba, CAP, part)
        else:
            yown[q] = y[0].reshape(n_ba, CAP, part)
        if d + DN_SLOTS < len(chunks):
            for copy in dn_copies(d + DN_SLOTS):
                copy.start()
        if late is not None:
            finish(*late)
        late = (q, kx)
        if d == 0 or d == last:
            finish(q, kx)
            late = None
        done = set()
        for qq, k in gives.get(d, []):
            if d == last and qq > 1 and qq - 2 not in done:
                blend(qq - 2)
                done.add(qq - 2)
            give(qq, k)
    for q in range(PARTS):
        if q not in done:
            blend(q)

    for buf, sems in ((stat_all, (stat_s, stat_r)), (note_all, (note_s, note_r)), (ld_all, (ld_s, ld_r))):
        everyone(buf, sems).wait_send()
    local_part = x_all.at[pl.ds(0, PARTS), :, :, pl.ds(0, part)]
    passes = x_all.at[pl.ds(0, PARTS * (nx - 1)), :, :, pl.ds(0, part)]
    for buf, sems in (
        (bs, (z_s, z_r)), (bs, (b_s, b_r)), (local_part, (c_s, c_r)), (passes, (x_s, x_r)),
        (passes, (f_s, f_r)), (xs, (q_s, q_r)), (ys, (p_s, p_r)), (d_send, (d_s, d_r)),
        (e_send, (e_s, e_r)),
    ):
        remote(buf, buf, sems, 0, partner).wait_send()
    for q in range(PARTS):
        leave(q).wait()


def shards(
    head_outputs,
    stream,
    adapter_down_factors,
    adapter_up_factors,
    norm_gain_vector,
    router_matrix,
    token_adapter_index,
    token_expert_index,
    gate_weight,
    up_weight,
    down_weight,
):
    toks, model_width = head_outputs.shape
    n_aa, n_ba = lax.axis_size("aa"), lax.axis_size("ba")
    nx = n_aa // CORES
    held = adapter_down_factors.shape[1]
    ff = gate_weight.shape[2]
    width = model_width // n_aa
    part = width // PARTS
    rows = n_ba * CAP
    nt = 2 if ff % 512 == 0 else ff // 128
    dma = pltpu.SemaphoreType.DMA
    vmem = pltpu.VMEM
    far = max(nx - 1, 1)

    def sems(n):
        return [dma((1,)), dma((max(n, 1),))]

    mixed, load = pl.pallas_call(
        functools.partial(layer, n_aa, n_ba, nt),
        out_shape=(
            jax.ShapeDtypeStruct((toks, width), BF16),
            jax.ShapeDtypeStruct((1, held // ADAPTER_RANK), F32),
        ),
        in_specs=[pl.BlockSpec(memory_space=pl.ANY)] * 11,
        out_specs=(pl.BlockSpec(memory_space=pl.ANY), pl.BlockSpec(memory_space=pltpu.VMEM)),
        scratch_shapes=[
            vmem((toks, model_width), BF16),
            vmem((toks, width), BF16),
            vmem((model_width, held), BF16),
            vmem((held, model_width), BF16),
            vmem((1, width), F32),
            vmem((E, width), BF16),
            vmem((1, toks), jnp.int32),
            vmem((2, toks), jnp.int32),
            vmem((PARTS, nx, toks, part), BF16),
            vmem((PARTS, nx, toks, part), BF16),
            vmem((PARTS, far, toks, part), BF16),
            vmem((PARTS, far, toks, part), BF16),
            vmem((n_aa, 2 * E, toks), F32),
            vmem((n_ba, 2 * E, toks), F32),
            vmem((n_ba, 8, held), F32),
            vmem((toks, width), F32),
            vmem((PARTS, E, CAP, part), BF16),
            vmem((rows, 128), F32),
            vmem((toks, rows), BF16),
            vmem((toks, rows), BF16),
            vmem((toks, 128), F32),
            vmem((toks, 128), F32),
            vmem((toks, width), BF16),
            vmem((PARTS * nx, n_ba, CAP, CORES * part), BF16),
            vmem((nt, rows, ff // nt), F32),
            vmem((nt, rows, ff // nt), F32),
            vmem((rows, ff), BF16),
            vmem((GU_DEPTH * nt, CORES * part, ff // nt), BF16),
            vmem((GU_DEPTH * nt, CORES * part, ff // nt), BF16),
            vmem((DN_SLOTS, CORES, ff, part), BF16),
            vmem((PARTS, nx, n_ba, CAP, part), BF16),
            vmem((PARTS, nx, n_ba, CAP, part), BF16),
            vmem((PARTS, n_ba, CAP, part), F32),
            vmem((far, n_ba, CAP, part), F32),
            vmem((PARTS, far, n_ba, CAP, part), BF16),
            vmem((PARTS, far, n_ba, CAP, part), BF16),
            vmem((PARTS, n_ba - 1, CAP, part), BF16),
            vmem((PARTS, n_ba, CAP, part), BF16),
            dma((8,)),
            dma((GU_DEPTH * nt, 2)),
            dma((DN_SLOTS, CORES)),
            dma((PARTS,)),
        ]
        + sems(PARTS * nx)
        + sems(PARTS * (nx - 1))
        + sems(1) * 3
        + sems(PARTS * (n_ba - 1))
        + sems(PARTS * (nx - 1))
        + sems(PARTS)
        + sems(PARTS * (nx - 1))
        + sems(PARTS * nx)
        + sems(PARTS * n_ba * (nx - 1))
        + sems(PARTS),
        compiler_params=pltpu.CompilerParams(
            collective_id=0, has_side_effects=True, vmem_limit_bytes=67043328
        ),
        name="layer",
    )(
        head_outputs, stream, adapter_down_factors, adapter_up_factors,
        norm_gain_vector[None, :], router_matrix.T, token_adapter_index[None, :],
        token_expert_index.T, gate_weight, up_weight, down_weight,
    )
    return (mixed, load.reshape(held // ADAPTER_RANK))


def solution(mesh):
    in_specs = (
        P("ba", None),
        P("ba", None),
        P(None, "aa"),
        P("aa", None),
        P(),
        P(),
        P("ba"),
        P("ba", None),
        P("ba", None, "aa"),
        P("ba", None, "aa"),
        P("ba", "aa", None),
    )
    out_specs = (P("ba", "aa"), P("aa"))
    return jax.shard_map(shards, mesh=mesh, in_specs=in_specs, out_specs=out_specs, check_vma=False)
```

time: 96.6 us -> 83.1 us (0.86)
  Pallas kernels: 92.4 us -> 79.4 us
    pallas_call x1, Pallas kernels: 92.4 us -> 79.4 us  [shards(): pl.pallas_call(functools.partial(layer, n_aa, n_ba, nt), out_shape=(jax.S...]
    squeeze x1 -> x0, local copies, waits for them, and re-layouts: 1.2 us -> none  [shards(): return (mixed, load[0, :held // ADAPTER_RANK])]
    unnamed x1 -> x2, local copies, waits for them, and re-layouts: 1.67 us -> 2.8 us
where the time goes in v2:
time: 83.1 us; the launch traced here: 82.8 us
  Pallas kernels  79.4 us (96%)
  local copies, waits for them, and re-layouts  2.8 us (3%)
    pallas_call x1, Pallas kernels, shards(): pl.pallas_call(functools.partial(layer, n_aa, n_ba, nt), out_shape=(jax.S...  79.4 us
    unnamed x2, local copies, waits for them, and re-layouts  2.8 us

profile of v2, /device:TPU:0, one launch (start us, length us, event | category | flops | bytes accessed | tf_op | source)
XLA Modules:
  0.0 82.8 jit_solution(4560165502570304615)
XLA Ops:
  0.6 79.4 %layer.1 = (bf16[128,1024]{1,0:T(8,128)(2,1)}, f32[1,8]{1,0:T(1,128)}) custom-call(bf16[128,4096]{1,0:T(8,128)(2,1)} %head_hbm.1, bf16[128,4096]{1,0:T(8,128)(2,1)} %stream_hbm.1, bf16[4096,128]{1,0:T(8,128)(2,1)} %down_hbm.1, bf16[128,4096]{1,0:T(8,128)(2,1)} %up_hbm.1, f32[1,4096]{1,0:T(1,128)} %bitcast.6, bf16[8,4096]{1,0:T(8,128)(2,1)} %bitcast.5, ...), custom_call_target="tpu_custom_call" | custom-call | tf_op jit(solution)/shard_map/layer/pallas_call | solution.py:531
  80.0 1.7 %copy.15 = bf16[128,1024]{1,0:T(8,128)(2,1)} copy(bf16[128,1024]{1,0:T(8,128)(2,1)} %get-tuple-element.8) | data formatting | bytes 524288
  81.7 1.1 %copy.16 = f32[8]{0:T(128)} copy(f32[8]{0:T(128)} %bitcast.9) | data formatting | bytes 64

commit v3 on v2

--- a/solution.py
+++ b/solution.py
@@ -322,13 +322,13 @@
         hooks.setdefault(min(it, steps - 1), []).append(functools.partial(fn, *args))
 
     def whole(it):
-        return -(-it // nt) * nt if it > 3 * nt else it
+        return it // nt * nt if it > 3 * nt else it
 
     for q in range(1, PARTS):
         need = groups.index((q, 0)) * nt
         for n, k in enumerate(arrival):
             due = -(-(264 * (q - 1) + 264 * (n + 1) // n_ba + 60) // 100) * nt // 2
-            hook(whole(min(max(due, 1), need)), forward, q, k)
+            hook(whole(min(max(due, 1), need - 1)), forward, q, k)
     for q in range(PARTS):
         for kx in far:
             need = groups.index((q, kx)) * nt

time: 83.1 us -> 80.7 us (0.971)
  Pallas kernels: 79.4 us -> 77 us
    pallas_call x1, Pallas kernels: 79.4 us -> 77 us  [shards(): pl.pallas_call(functools.partial(layer, n_aa, n_ba, nt), out_shape=(jax.S...]
where the time goes in v3:
time: 80.7 us; the launch traced here: 80.5 us
  Pallas kernels  77 us (95%)
  local copies, waits for them, and re-layouts  2.8 us (3%)
    pallas_call x1, Pallas kernels, shards(): pl.pallas_call(functools.partial(layer, n_aa, n_ba, nt), out_shape=(jax.S...  77 us
    unnamed x2, local copies, waits for them, and re-layouts  2.8 us

profile of v3, /device:TPU:0, one launch (start us, length us, event | category | flops | bytes accessed | tf_op | source)
XLA Modules:
  0.0 80.5 jit_solution(593365745445417772)
XLA Ops:
  0.6 77.0 %layer.1 = (bf16[128,1024]{1,0:T(8,128)(2,1)}, f32[1,8]{1,0:T(1,128)}) custom-call(bf16[128,4096]{1,0:T(8,128)(2,1)} %head_hbm.1, bf16[128,4096]{1,0:T(8,128)(2,1)} %stream_hbm.1, bf16[4096,128]{1,0:T(8,128)(2,1)} %down_hbm.1, bf16[128,4096]{1,0:T(8,128)(2,1)} %up_hbm.1, f32[1,4096]{1,0:T(1,128)} %bitcast.6, bf16[8,4096]{1,0:T(8,128)(2,1)} %bitcast.5, ...), custom_call_target="tpu_custom_call" | custom-call | tf_op jit(solution)/shard_map/layer/pallas_call | solution.py:531
  77.7 1.7 %copy.15 = bf16[128,1024]{1,0:T(8,128)(2,1)} copy(bf16[128,1024]{1,0:T(8,128)(2,1)} %get-tuple-element.8) | data formatting | bytes 524288
  79.3 1.1 %copy.16 = f32[8]{0:T(128)} copy(f32[8]{0:T(128)} %bitcast.9) | data formatting | bytes 64
